TPU v7x, 512 devices: a whole 4x4x16 slice. The times are simulated.
512 devices in a mesh: dp: 64 (over y_lo, z, core), mp: 8 (over y_hi, x).
Axes of the slice: x: 4, y: 4 (y_hi: 2, y_lo: 2; y = y_hi * 2 + y_lo), z: 16, core: 2. Of those that a mesh axis runs over, the one named last changes fastest.
Arguments:
- hidden_in: bfloat16 [32768, 4096], P('dp'), may hold values from -1.5 to 1.5
- w_query: bfloat16 [4096, 4096], P('dp', 'mp'), may hold values from -1 to 1
- w_key: bfloat16 [4096, 1024], P('dp', 'mp'), may hold values from -24 to 24
- w_value: bfloat16 [4096, 1024], P('dp', 'mp'), may hold values from -1 to 1
- w_out: bfloat16 [4096, 4096], P('dp', 'mp'), may hold values from -1 to 1
- value_weight: float32 [4096], P('mp'), may hold values from -0.09375 to 0.09375
- rewards: float32 [32768], P('dp'), may hold values from -0.6 to 0.6
- old_values: float32 [32768], P('dp'), may hold values from -6 to 6
- lengths: int32 [256], replicated, may hold values from 1 to 2048, 32768 in all
- terminal: int32 [256], replicated, may hold values 0 or 1
Outputs:
- value: float32 [32768], P('dp')
- advantage: float32 [32768], P('dp')
- value_loss: float32 [], replicated
All inputs are finite; a program needn't handle non-finite values.
Results may differ from a plain program's by a relative error of at most 0.012.
The roundings to bfloat16 on the way count: a program that leaves them out, or rounds other values in their place, can miss the bound.
Values may be sent and summed in bfloat16 or wider, within the bound.
A program may use at most 128 MiB of HBM per device.

v0:
```python
import jax
import jax.numpy as jnp
from jax import lax
from jax.sharding import PartitionSpec as P

HEAD = 128
discount = 0.999
trace_decay = 0.997
clip_range = 0.2
epsilon = 1e-05
rope_base = 500000.0


def sent_together(arrays, axis, dim, along):
    widths = [a.shape[along] for a in arrays]
    both = jnp.concatenate(arrays, axis=along)
    whole = lax.all_gather(both, axis, axis=dim, tiled=True)
    return tuple(jnp.split(whole, [sum(widths[:k]) for k in range(1, len(widths))], axis=along))


def from_everyone(array, axis):
    size = lax.axis_size(axis)
    return lax.all_to_all(
        jnp.broadcast_to(array[None], (size, *array.shape)), axis, 0, 0, tiled=True
    )


def of_everyone(array, axis):
    everything = from_everyone(array, axis)
    return jnp.sum(everything, axis=0)


def in_one(arrays, axis):
    ends = [0]
    for a in arrays:
        ends.append(ends[-1] + a.size)
    total = of_everyone(jnp.concatenate([a.ravel() for a in arrays]), axis)
    return tuple((total[b:e].reshape(a.shape) for a, b, e in zip(arrays, ends, ends[1:])))


def from_behind(array, axis, by):
    size = lax.axis_size(axis)
    pairs = [(i, i + by) for i in range(size) if 0 <= i + by < size]
    return lax.ppermute(array, axis, pairs)


def collected_together(array, axis):
    leaves = jax.tree.leaves(array)
    order = sorted(range(len(leaves)), key=lambda k: -leaves[k].size)
    width = (1, *leaves[order[0]].shape)[-1]
    lines = [
        jnp.pad(leaves[k].reshape(-1), (0, -leaves[k].size % width)).reshape(-1, width)
        for k in order
    ]
    both, at, found = (from_everyone(jnp.concatenate(lines), axis), 0, {})
    for k, line in zip(order, lines):
        slab = both[:, at : at + len(line)].reshape(len(both), -1)
        found[k] = slab[:, : leaves[k].size].reshape(-1, *leaves[k].shape)
        at += len(line)
    numbers = iter(range(len(leaves)))
    return jax.tree.map(lambda _: found[next(numbers)], array)


def joined_by_halves(pieces, combine):
    while len(jax.tree.leaves(pieces)[0]) > 1:
        pieces = jax.vmap(combine)(
            *(jax.tree.map(lambda part: part[side::2], pieces) for side in (0, 1))
        )
    return jax.tree.map(lambda part: part[0], pieces)


def prefix_2(array, axis, combine, identity):
    size, mine = (lax.axis_size(axis), lax.axis_index(axis))
    passed = jnp.arange(size) > mine

    def kept(part, zero, own):
        part = jnp.where(
            passed.reshape(-1, *(1 for _ in own.shape)), part, jnp.asarray(zero, own.dtype)
        )
        return part[::-1]

    pieces = collected_together(array, axis)
    return joined_by_halves(jax.tree.map(kept, pieces, identity, array), combine)


def rotate(states, positions):
    half = HEAD // 2
    freq = rope_base ** (-jnp.arange(half, dtype=jnp.float32) * 2.0 / HEAD)
    angles = positions[:, None] * freq[None, :]
    cosine = jnp.cos(angles)[:, None, :]
    sine = jnp.sin(angles)[:, None, :]
    first = states[..., :half]
    second = states[..., half:]
    return jnp.concatenate([first * cosine - second * sine, second * cosine + first * sine], -1)


def body(
    hidden_in, w_query, w_key, w_value, w_out, value_weight, rewards, old_values, lengths, terminal
):
    rows = hidden_in.shape[0]
    width = hidden_in.shape[1]
    states = hidden_in.astype(jnp.float32)
    normed = (states * lax.rsqrt(jnp.mean(states * states, 1, keepdims=True) + epsilon)).astype(
        jnp.bfloat16
    )
    pieces = sent_together((w_query, w_key, w_value, w_out), "dp", 0, 1)
    add_pieces = pieces[:3]
    summed = tuple(
        (jnp.dot(normed, piece, preferred_element_type=jnp.float32) for piece in add_pieces)
    )
    stored = pieces[3]
    query_sum, key_sum, value_sum, whole_out = summed + (stored,)
    position_ids = lax.axis_index("dp") * rows + jnp.arange(rows, dtype=jnp.int32)
    positions = position_ids.astype(jnp.float32)
    local_heads = w_query.shape[1] // HEAD
    local_kv = w_key.shape[1] // HEAD
    group = local_heads // local_kv
    query = rotate(query_sum.reshape(rows, local_heads, HEAD), positions).astype(jnp.bfloat16)
    key = rotate(key_sum.reshape(rows, local_kv, HEAD), positions).astype(jnp.bfloat16)
    values_proj = value_sum.astype(jnp.bfloat16).reshape(rows, local_kv, HEAD)
    ends = jnp.cumsum(lengths)
    matches = ends[None, :] - 1 == position_ids[:, None]
    finished = jnp.any(matches, 1).astype(jnp.float32)
    stopped = jnp.sum(jnp.where(matches, terminal[None, :], 0), 1).astype(jnp.float32)
    episode = jnp.sum((ends[None, :] <= position_ids[:, None]).astype(jnp.int32), 1)
    order = jnp.arange(rows, dtype=jnp.int32)
    same_episode = episode[None, :] == episode[:, None]
    allowed = (order[None, :] <= order[:, None]) & same_episode
    scores = jnp.einsum(
        "tkgd,skd->kgts",
        query.reshape(rows, local_kv, group, HEAD),
        key,
        preferred_element_type=jnp.float32,
    ) * (1.0 / HEAD**0.5)
    masked = jnp.where(allowed[None, None], scores, -1e30)
    largest = jnp.max(masked, -1, keepdims=True)
    expon = jnp.where(allowed[None, None], jnp.exp(masked - largest), 0.0)
    probs = (expon / jnp.sum(expon, -1, keepdims=True)).astype(jnp.bfloat16)
    output = jnp.einsum("kgts,skd->tkgd", probs, values_proj, preferred_element_type=jnp.float32)
    attended = output.astype(jnp.bfloat16).reshape(rows, local_heads * HEAD)
    all_heads = lax.all_gather(attended, "mp", axis=1, tiled=True)
    projected = jnp.dot(all_heads, whole_out, preferred_element_type=jnp.float32)
    feature_count = w_out.shape[1]
    own_states = lax.dynamic_slice_in_dim(
        states, lax.axis_index("mp") * feature_count, feature_count, 1
    )
    residual = own_states + projected
    square_sum, head_sum = in_one(
        (jnp.sum(residual * residual, 1), jnp.sum(residual * value_weight[None, :], 1)), "mp"
    )
    value = head_sum * lax.rsqrt(square_sum / width + epsilon)
    following = from_behind(old_values[:1], "dp", -1)
    next_old = jnp.concatenate([old_values[1:], following])
    booted = jnp.where(finished > 0, (1.0 - stopped) * old_values, next_old)
    delta = rewards + discount * booted - old_values
    keep_rate = discount * trace_decay
    spacing = (order[None, :] - order[:, None]).astype(jnp.float32)
    forward_mask = (spacing >= 0.0) & same_episode
    decay_matrix = jnp.where(
        forward_mask, jnp.power(jnp.float32(keep_rate), jnp.maximum(spacing, 0.0)), 0.0
    )
    local_part = jnp.dot(decay_matrix, delta, precision=lax.Precision.HIGHEST)
    remaining = (rows - order).astype(jnp.float32)
    reach = jnp.where(episode == episode[-1], jnp.power(jnp.float32(keep_rate), remaining), 0.0) * (
        1.0 - finished[-1]
    )

    def compose(earlier, later_map):
        return (later_map[0] + later_map[1] * earlier[0], later_map[1] * earlier[1])

    prefix = prefix_2(
        (local_part[:1], reach[:1]),
        "dp",
        compose,
        (jnp.zeros((1,), jnp.float32), jnp.ones((1,), jnp.float32)),
    )
    incoming = prefix[0][0]
    advantage = local_part + reach * incoming
    returns = advantage + old_values
    clipped = old_values + jnp.clip(value - old_values, -clip_range, clip_range)
    terms = jnp.maximum((value - returns) ** 2, (clipped - returns) ** 2)
    total_loss = of_everyone(jnp.sum(terms), "dp")
    value_loss = 0.5 * total_loss / (rows * lax.axis_size("dp"))
    return (value, advantage, value_loss)


def solution(mesh):
    return jax.shard_map(
        body,
        mesh=mesh,
        in_specs=(
            P("dp", None),
            P("dp", "mp"),
            P("dp", "mp"),
            P("dp", "mp"),
            P("dp", "mp"),
            P("mp"),
            P("dp"),
            P("dp"),
            P(),
            P(),
        ),
        out_specs=(P("dp"), P("dp"), P()),
        check_vma=False,
    )
```

profile of v0, /device:TPU:1, one launch (start us, length us, event | category | flops | bytes accessed | tf_op | source)
XLA Modules:
  0.0 308.6 jit_solution(11443152681858207137)
XLA Ops:
  7.2 1.6 pad_maximum_fusion
  8.9 1.0 reduce-window.9
  10.0 6.5 %copy.47 = bf16[512,4096]{0,1:T(8,128)(2,1)} copy(bf16[512,4096]{1,0:T(8,128)(2,1)} %param.10) | data formatting | bytes 8388608 | tf_op args[0]
  16.5 0.1 slice_reduce_fusion.2
  16.7 0.3 fusion.29
  17.0 3.1 %multiply_reduce_fusion = f32[512]{0:T(512)S(1)} fusion(bf16[512,4096]{0,1:T(8,128)(2,1)} %copy.47), kind=kLoop, calls=%fused_computation.1 | loop fusion | flops 6290944 | bytes 4196352 | tf_op jit(solution)/shard_map/reduce_sum | solution.py:103
  20.2 0.2 compare_and_fusion.1
  20.4 1.0 multiply_cosine_fusion
  21.4 125.4 %all-gather.3.cloned.1.call-done = bf16[4096,1280]{1,0:T(8,128)(2,1)} async-done(((bf16[64,1280]{1,0:T(8,128)(2,1)}), bf16[4096,1280]{1,0:T(8,128)(2,1)}) %all-gather.3.cloned.1.call-update) | async-done | bytes 10485776 | tf_op jit(solution)/shard_map/all_gather | solution.py:17
  146.8 3.6 %fusion.17 = f32[512,1,128]{0,2,1:T(8,128)S(1)} fusion(f32[512]{0:T(512)S(1)} %add_rsqrt_fusion, bf16[512,4096]{0,1:T(8,128)(2,1)} %copy.47, bf16[4096,1280]{1,0:T(8,128)(2,1)} %all-gather.3.cloned.1.call-done), kind=kOutput, calls=%fused_computation.20 | convolution fusion | flops 543162368 | bytes 5507072 | tf_op jit(solution)/shard_map/dot_general | solution.py:109
  150.4 0.6 fusion.49
  151.0 4.7 %fusion.2 = f32[512,512]{0,1:T(8,128)S(1)} fusion(bf16[4096,1280]{1,0:T(8,128)(2,1)} %all-gather.3.cloned.1.call-done, f32[512]{0:T(512)S(1)} %add_rsqrt_fusion, bf16[512,4096]{0,1:T(8,128)(2,1)S(1)} %copy-done), kind=kOutput, calls=%fused_computation.4 | convolution fusion | flops 2153775104 | bytes 9439232 | tf_op jit(solution)/shard_map/dot_general | solution.py:109
  155.7 0.1 fusion.60
  155.8 0.3 copy.63
  156.1 0.3 copy.62
  156.5 0.3 subtract_convert_fusion
  156.8 1.2 fusion.4
  158.0 2.1 copy-done.1
  160.1 1.0 fusion.7
  161.1 7.6 %fusion.14 = bf16[128,4,512]{2,0,1:T(8,128)(2,1)} fusion(f32[4,512]{1,0:T(4,128)S(1)} %fusion.7, f32[4,512]{1,0:T(4,128)S(1)} %get-tuple-element.34, f32[512,512,4]{1,0,2:T(8,128)} %copy-done.1, pred[512,512]{0,1:T(8,128)(4,1)S(1)} %compare_and_fusion.1, f32[512]{0:T(512)S(1)} %copy-done.4, bf16[512,4096]{0,1:T(8,128)(2,1)} %copy.47, ...), kind=kOutput, calls=%fused_computation.19 | convolution fusion | flops 818216960 | bytes 10242048 | tf_op jit(solution)/shard_map/kgts,skd->tkgd/dot_general | solution.py:139
  168.8 0.5 slice.142
  169.3 2.2 collective-permute-start
  171.5 0.7 slice.143
  172.3 0.2 compare_reduce_fusion
  172.5 0.6 slice.144
  173.7 0.7 select_multiply_fusion
  174.4 0.5 slice.146
  175.0 0.7 fusion.52
  175.7 1.1 fusion.22
  176.8 0.5 slice.145
  177.3 1.4 maximum_bitcast_fusion.2
  178.7 0.6 broadcast_in_dim.56
  179.3 9.7 %all-to-all-start.1 = ((f32[64,2,1]{1,2,0:T(1,128)}), f32[64,2,1]{1,2,0:T(1,128)S(1)}, u32[]{:S(2)}, u32[]{:S(2)}) async-start(f32[64,2,1]{1,2,0:T(1,128)} %broadcast_in_dim.56), calls=%async_computation.1 | async-start | bytes 65536 | tf_op jit(solution)/shard_map/all_to_all | solution.py:23
  189.0 6.7 %convert_element_type.52 = f32[512,4096]{0,1:T(8,128)} convert(bf16[512,4096]{0,1:T(8,128)(2,1)} %copy.47) | non-fusion elementwise | flops 2097152 | bytes 12582912 | tf_op jit(solution)/shard_map/convert_element_type | solution.py:102
  195.8 6.6 %all-to-all-done.1 = f32[64,2,1]{1,2,0:T(1,128)S(1)} async-done(((f32[64,2,1]{1,2,0:T(1,128)}), f32[64,2,1]{1,2,0:T(1,128)S(1)}, u32[]{:S(2)}, u32[]{:S(2)}) %all-to-all-start.1) | async-done | bytes 544 | tf_op jit(solution)/shard_map/all_to_all | solution.py:23
  202.3 1.1 slice_reduce_fusion
  203.4 0.1 slice.156
  203.6 0.1 slice.151
  203.7 0.1 slice.153
  203.8 0.1 slice.148
  203.9 0.1 slice.152
  204.0 0.1 slice.157
  204.1 0.1 slice.149
  204.2 0.1 slice.154
  204.3 0.1 slice.161
  204.4 0.1 slice.158
  204.6 0.1 slice.159
  204.7 0.1 slice.155
  204.8 0.1 slice.165
  204.9 0.1 slice.162
  205.0 0.1 slice.163
  205.1 0.1 slice.160
  205.3 0.1 slice.166
  206.0 45.3 %all-gather.5.cloned.1.call-done = bf16[512,4096]{0,1:T(8,128)(2,1)} async-done(((bf16[512,512]{0,1:T(8,128)(2,1)}), bf16[512,4096]{0,1:T(8,128)(2,1)}) %all-gather.5.cloned.1.call-update) | async-done | bytes 4194320 | tf_op jit(solution)/shard_map/all_gather | solution.py:141
  251.3 6.1 %multiply_reduce_fusion.2 = (f32[512]{0:T(512)S(1)}, f32[512]{0:T(512)S(1)}) fusion(f32[512]{0:T(512)S(1)} %copy-done.7, bf16[512,4096]{0,1:T(8,128)(2,1)} %all-gather.5.cloned.1.call-done, bf16[4096,1280]{1,0:T(8,128)(2,1)} %all-gather.3.cloned.1.call-done, f32[512,4096]{0,1:T(8,128)} %convert_element_type.52, s32[]{:T(128)S(6)} %select_n.49), kind=kOutput, calls=%fused_computation.33 | convolution fusion | flops 2148793344 | bytes 9443332 | tf_op jit(solution)/shard_map/dot_general | solution.py:142
  257.4 0.6 broadcast_in_dim.51
  258.0 3.3 %all-to-all-start = ((f32[8,1,1024]{2,1,0:T(1,128)}), f32[8,1,1024]{2,1,0:T(1,128)S(1)}, u32[]{:S(2)}, u32[]{:S(2)}) async-start(f32[8,1,1024]{2,1,0:T(1,128)} %broadcast_in_dim.51), calls=%async_computation | async-start | bytes 65536 | tf_op jit(solution)/shard_map/all_to_all | solution.py:23
  261.4 0.6 fusion.61
  262.0 0.6 slice.174
  264.5 3.4 %all-to-all-done = f32[8,1,1024]{2,1,0:T(1,128)S(1)} async-done(((f32[8,1,1024]{2,1,0:T(1,128)}), f32[8,1,1024]{2,1,0:T(1,128)S(1)}, u32[]{:S(2)}, u32[]{:S(2)}) %all-to-all-start) | async-done | bytes 32800 | tf_op jit(solution)/shard_map/all_to_all | solution.py:23
  268.0 2.0 maximum_reduce_fusion
  269.9 0.7 broadcast_in_dim.96
  270.6 28.7 %all_to_all.17 = f32[64,1,1]{2,1,0:T(1,128)S(1)} all-to-all(f32[64,1,1]{2,1,0:T(1,128)S(1)} %broadcast_in_dim.96), channel_id=1, replica_groups=mesh['dp'=64,'mp'=8] {'dp'}, dimensions={0} | all-to-all | bytes 512 | tf_op jit(solution)/shard_map/all_to_all | solution.py:23
  299.3 0.7 reduce_sum.89
  (44 shorter events, 1.2 us)
Async XLA Ops:
  7.2 139.6 %all-gather.3.cloned.1.call-start = ((), (), s32[]{:S(2)}) async-start(), calls=%async_computation.3 | async-start | bytes 10649600 | tf_op jit(solution)/shard_map/all_gather | solution.py:17
  8.8 242.5 %all-gather.5.cloned.1.call-start = ((), (), s32[]{:S(2)}) async-start(), calls=%async_computation.4 | async-start | bytes 4718592 | tf_op jit(solution)/shard_map/all_gather | solution.py:141
  10.0 6.7 %copy-start.6 = (s32[256]{0:T(256)S(1)}, s32[256]{0:T(256)}, u32[]{:S(2)}) copy-start(s32[256]{0:T(256)} %param.19) | copy-start | bytes 3076
  20.1 130.8 %copy-start.3 = (f32[512]{0:T(512)}, f32[512]{0:T(512)S(1)}, u32[]{:S(2)}) copy-start(f32[512]{0:T(512)S(1)} %add_rsqrt_fusion) | copy-start | bytes 6148
  146.8 4.2 %copy-start = (bf16[512,4096]{0,1:T(8,128)(2,1)S(1)}, bf16[512,4096]{0,1:T(8,128)(2,1)}, u32[]{:S(2)}) copy-start(bf16[512,4096]{0,1:T(8,128)(2,1)} %copy.47) | copy-start | bytes 12582916
  156.8 4.4 %copy-start.4 = (f32[512]{0:T(512)S(1)}, f32[512]{0:T(512)}, u32[]{:S(2)}) copy-start(f32[512]{0:T(512)} %copy-done.3) | copy-start | bytes 6148
  158.0 2.1 copy-start.1
  161.1 7.7 %copy-start.2 = (f32[512]{0:T(512)S(1)}, f32[512]{0:T(512)}, u32[]{:S(2)}) copy-start(f32[512]{0:T(512)} %param.17) | copy-start | bytes 6148
  161.1 13.8 %copy-start.5 = (f32[512]{0:T(512)S(1)}, f32[512]{0:T(512)}, u32[]{:S(2)}) copy-start(f32[512]{0:T(512)} %param.16) | copy-start | bytes 6148
  169.3 5.6 %collective-permute-start = (f32[1]{0:T(128)}, f32[1]{0:T(128)}, u32[]{:S(2)}, u32[]{:S(2)}) collective-permute-start(f32[1]{0:T(128)} %slice.142), channel_id=1, source_target_pairs={{8,0},{16,8},{24,16},{32,24},{40,32},{48,40},{56,48},{64,56},{72,6... | collective-permute-start | bytes 20 | tf_op jit(solution)/shard_map/ppermute | solution.py:44
  179.3 23.1 %all-to-all-start.1 = ((f32[64,2,1]{1,2,0:T(1,128)}), f32[64,2,1]{1,2,0:T(1,128)S(1)}, u32[]{:S(2)}, u32[]{:S(2)}) async-start(f32[64,2,1]{1,2,0:T(1,128)} %broadcast_in_dim.56), calls=%async_computation.1 | async-start | bytes 65536 | tf_op jit(solution)/shard_map/all_to_all | solution.py:23
  189.0 62.3 %copy-start.7 = (f32[512]{0:T(512)S(1)}, f32[512]{0:T(512)}, u32[]{:S(2)}) copy-start(f32[512]{0:T(512)} %param.15) | copy-start | bytes 6148
  258.0 9.9 %all-to-all-start = ((f32[8,1,1024]{2,1,0:T(1,128)}), f32[8,1,1024]{2,1,0:T(1,128)S(1)}, u32[]{:S(2)}, u32[]{:S(2)}) async-start(f32[8,1,1024]{2,1,0:T(1,128)} %broadcast_in_dim.51), calls=%async_computation | async-start | bytes 65536 | tf_op jit(solution)/shard_map/all_to_all | solution.py:23
Sparse Core Ops, SparseCore 0:
  10.1 136.5 all-gather.2
  168.9 82.2 all-gather.4
where the time goes:
time: 309 us
  waiting for transfers between devices  181 us (59%)
  blocking collectives  28.7 us (9%)
  matrix products  24.4 us (8%)
  other arithmetic  21.7 us (7%)
  local copies, waits for them, and re-layouts  19.1 us (6%)
  between operations  18.7 us (6%)
  starting transfers between devices  15.3 us (5%)
    all_gather x1, waiting for transfers between devices, sent_together(): whole = lax.all_gather(both, axis, axis=dim, tiled=True)  125 us
    all_gather x1, waiting for transfers between devices, body(): all_heads = lax.all_gather(attended, 'mp', axis=1, tiled=True)  45.3 us
    all_to_all x1, blocking collectives, from_everyone(): lax.all_to_all(jnp.broadcast_to(array[None], (size, *array.shape)), axis,...  28.7 us
    all_to_all x2, starting transfers between devices, from_everyone(): lax.all_to_all(jnp.broadcast_to(array[None], (size, *array.shape)), axis,...  13.1 us
    all_to_all x2, waiting for transfers between devices, from_everyone(): lax.all_to_all(jnp.broadcast_to(array[None], (size, *array.shape)), axis,...  9.99 us
    unnamed x19, local copies, waits for them, and re-layouts  9.27 us
    dot_general x2, matrix products, body(): jnp.dot(normed, piece, preferred_element_type=jnp.float32)  8.31 us
    dot_general x1, matrix products, body(): jnp.einsum('kgts,skd->tkgd', probs, values_proj, preferred_element_type=j...  7.65 us
  transfers between devices with their start and end apart: 5, of which 4 were waited for; matrix products, arithmetic and copies ran while one was open for 10% of the time, Pallas kernels for 0%

commit v1 on v0

--- a/solution.py
+++ b/solution.py
@@ -138,7 +138,9 @@
     probs = (expon / jnp.sum(expon, -1, keepdims=True)).astype(jnp.bfloat16)
     output = jnp.einsum("kgts,skd->tkgd", probs, values_proj, preferred_element_type=jnp.float32)
     attended = output.astype(jnp.bfloat16).reshape(rows, local_heads * HEAD)
-    all_heads = lax.all_gather(attended, "mp", axis=1, tiled=True)
+    all_heads = jnp.concatenate(
+        lax.all_to_all(jnp.stack([attended] * lax.axis_size("mp")), "mp", 0, 0), axis=1
+    )
     projected = jnp.dot(all_heads, whole_out, preferred_element_type=jnp.float32)
     feature_count = w_out.shape[1]
     own_states = lax.dynamic_slice_in_dim(

time: 309 us -> 296 us (0.958)
  waiting for transfers between devices: 181 us -> 140 us
  starting transfers between devices: 15.3 us -> 42.8 us
  blocking collectives: 28.7 us -> 23.9 us
  local copies, waits for them, and re-layouts: 19.1 us -> 22.8 us
    all_gather x1 -> x0, waiting for transfers between devices: 45.3 us -> none  [body(): all_heads = lax.all_gather(attended, 'mp', axis=1, tiled=True)]
    all_to_all x0 -> x1, waiting for transfers between devices: none -> 40.8 us  [body(): lax.all_to_all(jnp.stack([attended] * lax.axis_size('mp')), 'mp', 0, 0)]
    all_gather x1, waiting for transfers between devices: 125 us -> 95.9 us  [sent_together(): whole = lax.all_gather(both, axis, axis=dim, tiled=True)]
    all_to_all x2, starting transfers between devices: 13.1 us -> 27.9 us  [from_everyone(): lax.all_to_all(jnp.broadcast_to(array[None], (size, *array.shape)), axis,...]
    ppermute x1, starting transfers between devices: 2.18 us -> 8.74 us  [from_behind(): return lax.ppermute(array, axis, pairs)]
    all_to_all x2, waiting for transfers between devices: 9.99 us -> 3.51 us  [from_everyone(): lax.all_to_all(jnp.broadcast_to(array[None], (size, *array.shape)), axis,...]
    all_to_all x0 -> x1, starting transfers between devices: none -> 6.11 us  [body(): lax.all_to_all(jnp.stack([attended] * lax.axis_size('mp')), 'mp', 0, 0)]
    all_to_all x1, blocking collectives: 28.7 us -> 23.9 us  [from_everyone(): lax.all_to_all(jnp.broadcast_to(array[None], (size, *array.shape)), axis,...]
  transfers between devices with their start and end apart: 5 -> 5, of which waited for: 4 -> 3; matrix products, arithmetic and copies ran while one was open for 10% -> 18% of each run, Pallas kernels for 0% -> 0%
where the time goes in v1:
time: 296 us; the launch traced here: 295 us
  waiting for transfers between devices  140 us (47%)
  starting transfers between devices  42.8 us (14%)
  matrix products  24.2 us (8%)
  blocking collectives  23.9 us (8%)
  other arithmetic  22.9 us (8%)
  local copies, waits for them, and re-layouts  22.8 us (8%)
  between operations  18.6 us (6%)
    all_gather x1, waiting for transfers between devices, sent_together(): whole = lax.all_gather(both, axis, axis=dim, tiled=True)  95.9 us
    all_to_all x1, waiting for transfers between devices, body(): lax.all_to_all(jnp.stack([attended] * lax.axis_size('mp')), 'mp', 0, 0)  40.8 us
    all_to_all x2, starting transfers between devices, from_everyone(): lax.all_to_all(jnp.broadcast_to(array[None], (size, *array.shape)), axis,...  27.9 us
    all_to_all x1, blocking collectives, from_everyone(): lax.all_to_all(jnp.broadcast_to(array[None], (size, *array.shape)), axis,...  23.9 us
    unnamed x13, local copies, waits for them, and re-layouts  9.23 us
    ppermute x1, starting transfers between devices, from_behind(): return lax.ppermute(array, axis, pairs)  8.74 us
    dot_general x2, matrix products, body(): jnp.dot(normed, piece, preferred_element_type=jnp.float32)  8.3 us
    convert_element_type x1, other arithmetic, body(): states = hidden_in.astype(jnp.float32)  6.73 us
  transfers between devices with their start and end apart: 5, of which 3 were waited for; matrix products, arithmetic and copies ran while one was open for 18% of the time, Pallas kernels for 0%

profile of v1, /device:TPU:1, one launch (start us, length us, event | category | flops | bytes accessed | tf_op | source)
XLA Modules:
  0.0 295.5 jit_solution(449109743966171744)
XLA Ops:
  7.2 1.6 pad_maximum_fusion
  8.8 1.2 slice.142
  10.0 8.7 %collective-permute-start = (f32[1]{0:T(128)}, f32[1]{0:T(128)}, u32[]{:S(2)}, u32[]{:S(2)}) collective-permute-start(f32[1]{0:T(128)} %slice.142), channel_id=1, source_target_pairs={{8,0},{16,8},{24,16},{32,24},{40,32},{48,40},{56,48},{64,56},{72,6... | collective-permute-start | bytes 20 | tf_op jit(solution)/shard_map/ppermute | solution.py:44
  18.8 0.8 slice.141
  19.5 1.0 reduce-window.9
  20.6 0.1 slice_reduce_fusion.2
  20.8 1.0 fusion.29
  21.8 0.7 slice.143
  22.4 0.2 compare_reduce_fusion
  22.7 0.6 slice.144
  23.9 0.6 select_multiply_fusion
  24.6 0.5 slice.146
  25.1 6.5 %copy.48 = bf16[512,4096]{0,1:T(8,128)(2,1)} copy(bf16[512,4096]{1,0:T(8,128)(2,1)} %param.10) | data formatting | bytes 8388608 | tf_op args[0]
  31.6 3.2 %multiply_reduce_fusion = f32[512]{0:T(512)S(1)} fusion(bf16[512,4096]{0,1:T(8,128)(2,1)} %copy.48), kind=kLoop, calls=%fused_computation.1 | loop fusion | flops 6290944 | bytes 4196352 | tf_op jit(solution)/shard_map/reduce_sum | solution.py:103
  34.8 0.2 compare_and_fusion.1
  35.1 1.0 multiply_cosine_fusion
  36.1 0.6 fusion.52
  36.7 1.1 fusion.22
  37.8 0.5 slice.145
  38.4 1.4 maximum_bitcast_fusion.2
  39.7 0.6 broadcast_in_dim.56
  40.3 11.3 %all-to-all-start.2 = ((f32[64,2,1]{1,2,0:T(1,128)}), f32[64,2,1]{1,2,0:T(1,128)S(1)}, u32[]{:S(2)}, u32[]{:S(2)}) async-start(f32[64,2,1]{1,2,0:T(1,128)} %broadcast_in_dim.56), calls=%async_computation.2 | async-start | bytes 65536 | tf_op jit(solution)/shard_map/all_to_all | solution.py:23
  51.7 95.9 %all-gather.2.cloned.1.call-done = bf16[4096,1280]{1,0:T(8,128)(2,1)} async-done(((bf16[64,1280]{1,0:T(8,128)(2,1)}), bf16[4096,1280]{1,0:T(8,128)(2,1)}) %all-gather.2.cloned.1.call-update) | async-done | bytes 10485776 | tf_op jit(solution)/shard_map/all_gather | solution.py:17
  147.6 3.6 %fusion.17 = f32[512,1,128]{0,2,1:T(8,128)S(1)} fusion(f32[512]{0:T(512)S(1)} %add_rsqrt_fusion, bf16[512,4096]{0,1:T(8,128)(2,1)} %copy.48, bf16[4096,1280]{1,0:T(8,128)(2,1)} %all-gather.2.cloned.1.call-done), kind=kOutput, calls=%fused_computation.20 | convolution fusion | flops 543162368 | bytes 5507072 | tf_op jit(solution)/shard_map/dot_general | solution.py:109
  151.2 1.2 fusion.49
  152.4 4.7 %fusion.2 = f32[512,512]{0,1:T(8,128)S(1)} fusion(bf16[4096,1280]{1,0:T(8,128)(2,1)} %all-gather.2.cloned.1.call-done, f32[512]{0:T(512)S(1)} %add_rsqrt_fusion, bf16[512,4096]{0,1:T(8,128)(2,1)S(1)} %copy-done), kind=kOutput, calls=%fused_computation.4 | convolution fusion | flops 2153775104 | bytes 9439232 | tf_op jit(solution)/shard_map/dot_general | solution.py:109
  157.1 0.1 fusion.60
  157.2 0.3 copy.64
  157.5 0.3 copy.63
  157.9 0.3 subtract_convert_fusion
  158.2 2.0 fusion.4
  160.2 2.1 copy-done.1
  162.3 1.0 fusion.7
  163.3 6.6 %fusion.14 = bf16[128,4,512]{2,0,1:T(8,128)(2,1)S(1)} fusion(f32[4,512]{1,0:T(4,128)S(1)} %fusion.7, f32[4,512]{1,0:T(4,128)S(1)} %get-tuple-element.34, f32[512,512,4]{1,0,2:T(8,128)} %copy-done.1, pred[512,512]{0,1:T(8,128)(4,1)S(1)} %compare_and_fusion.1, f32[512]{0:T(512)S(1)} %add_rsqrt_fusion, bf16[512,4096]{0,1:T(8,128)(2,1)} %copy.48, ...), kind=kOutput, calls=%fused_computation.19 | convolution fusion | flops 818216960 | bytes 10242048 | tf_op jit(solution)/shard_map/kgts,skd->tkgd/dot_general | solution.py:139
  170.0 2.4 stack.3
  172.4 6.1 %all-to-all-start = ((bf16[8,512,512]{1,2,0:T(8,128)(2,1)}), bf16[8,512,512]{1,2,0:T(8,128)(2,1)}, u32[]{:S(2)}, u32[]{:S(2)}) async-start(bf16[8,512,512]{1,2,0:T(8,128)(2,1)} %stack.3), calls=%async_computation | async-start | bytes 8388608 | tf_op jit(solution)/shard_map/all_to_all | solution.py:142
  178.5 6.7 %convert_element_type.52 = f32[512,4096]{0,1:T(8,128)} convert(bf16[512,4096]{0,1:T(8,128)(2,1)} %copy.48) | non-fusion elementwise | flops 2097152 | bytes 12582912 | tf_op jit(solution)/shard_map/convert_element_type | solution.py:102
  185.2 1.1 slice_reduce_fusion
  186.4 0.1 slice.156
  186.5 0.1 slice.151
  186.6 0.1 slice.153
  186.7 0.1 slice.148
  186.9 0.1 slice.152
  187.0 0.1 slice.157
  187.1 0.1 slice.149
  187.1 0.1 slice.154
  187.2 0.1 slice.161
  187.4 0.1 slice.158
  187.5 0.1 slice.159
  187.6 0.1 slice.155
  187.7 0.1 slice.165
  187.8 0.1 slice.162
  188.0 0.1 slice.160
  188.9 40.8 %all-to-all-done = bf16[8,512,512]{1,2,0:T(8,128)(2,1)} async-done(((bf16[8,512,512]{1,2,0:T(8,128)(2,1)}), bf16[8,512,512]{1,2,0:T(8,128)(2,1)}, u32[]{:S(2)}, u32[]{:S(2)}) %all-to-all-start) | async-done | bytes 4194336 | tf_op jit(solution)/shard_map/all_to_all | solution.py:142
  229.7 6.1 %multiply_reduce_fusion.2 = (f32[512]{0:T(512)S(1)}, f32[512]{0:T(512)S(1)}) fusion(f32[512]{0:T(512)S(1)} %copy-done.4, bf16[512,4096]{0,1:T(8,128)(2,1)} %bitcast.15, bf16[4096,1280]{1,0:T(8,128)(2,1)} %all-gather.2.cloned.1.call-done, f32[512,4096]{0,1:T(8,128)} %convert_element_type.52, s32[]{:T(128)S(6)} %select_n.49), kind=kOutput, calls=%fused_computation.33 | convolution fusion | flops 2148793344 | bytes 9443332 | tf_op jit(solution)/shard_map/dot_general | solution.py:144
  235.8 0.6 broadcast_in_dim.51
  236.5 16.6 %all-to-all-start.1 = ((f32[8,1,1024]{2,1,0:T(1,128)}), f32[8,1,1024]{2,1,0:T(1,128)S(1)}, u32[]{:S(2)}, u32[]{:S(2)}) async-start(f32[8,1,1024]{2,1,0:T(1,128)} %broadcast_in_dim.51), calls=%async_computation.1 | async-start | bytes 65536 | tf_op jit(solution)/shard_map/all_to_all | solution.py:23
  253.1 0.6 fusion.61
  253.6 0.6 slice.174
  256.2 3.5 %all-to-all-done.1 = f32[8,1,1024]{2,1,0:T(1,128)S(1)} async-done(((f32[8,1,1024]{2,1,0:T(1,128)}), f32[8,1,1024]{2,1,0:T(1,128)S(1)}, u32[]{:S(2)}, u32[]{:S(2)}) %all-to-all-start.1) | async-done | bytes 32800 | tf_op jit(solution)/shard_map/all_to_all | solution.py:23
  259.7 1.9 maximum_reduce_fusion
  261.6 0.7 broadcast_in_dim.96
  262.3 23.9 %all_to_all.22 = f32[64,1,1]{2,1,0:T(1,128)S(1)} all-to-all(f32[64,1,1]{2,1,0:T(1,128)S(1)} %broadcast_in_dim.96), channel_id=1, replica_groups=mesh['dp'=64,'mp'=8] {'dp'}, dimensions={0} | all-to-all | bytes 512 | tf_op jit(solution)/shard_map/all_to_all | solution.py:23
  286.2 0.7 reduce_sum.89
  (38 shorter events, 1.2 us)
Async XLA Ops:
  7.2 140.4 %all-gather.2.cloned.1.call-start = ((), (), s32[]{:S(2)}) async-start(), calls=%async_computation.4 | async-start | bytes 10649600 | tf_op jit(solution)/shard_map/all_gather | solution.py:17
  10.0 26.0 %collective-permute-start = (f32[1]{0:T(128)}, f32[1]{0:T(128)}, u32[]{:S(2)}, u32[]{:S(2)}) collective-permute-start(f32[1]{0:T(128)} %slice.142), channel_id=1, source_target_pairs={{8,0},{16,8},{24,16},{32,24},{40,32},{48,40},{56,48},{64,56},{72,6... | collective-permute-start | bytes 20 | tf_op jit(solution)/shard_map/ppermute | solution.py:44
  31.6 4.5 %copy-start.2 = (f32[512]{0:T(512)S(1)}, f32[512]{0:T(512)}, u32[]{:S(2)}) copy-start(f32[512]{0:T(512)} %param.17) | copy-start | bytes 6148
  31.6 4.5 %copy-start.3 = (f32[512]{0:T(512)S(1)}, f32[512]{0:T(512)}, u32[]{:S(2)}) copy-start(f32[512]{0:T(512)} %param.16) | copy-start | bytes 6148
  40.3 129.6 %all-to-all-start.2 = ((f32[64,2,1]{1,2,0:T(1,128)}), f32[64,2,1]{1,2,0:T(1,128)S(1)}, u32[]{:S(2)}, u32[]{:S(2)}) async-start(f32[64,2,1]{1,2,0:T(1,128)} %broadcast_in_dim.56), calls=%async_computation.2 | async-start | bytes 65536 | tf_op jit(solution)/shard_map/all_to_all | solution.py:23
  147.6 4.8 %copy-start = (bf16[512,4096]{0,1:T(8,128)(2,1)S(1)}, bf16[512,4096]{0,1:T(8,128)(2,1)}, u32[]{:S(2)}) copy-start(bf16[512,4096]{0,1:T(8,128)(2,1)} %copy.48) | copy-start | bytes 12582916
  160.2 2.1 copy-start.1
  172.4 57.3 %all-to-all-start = ((bf16[8,512,512]{1,2,0:T(8,128)(2,1)}), bf16[8,512,512]{1,2,0:T(8,128)(2,1)}, u32[]{:S(2)}, u32[]{:S(2)}) async-start(bf16[8,512,512]{1,2,0:T(8,128)(2,1)} %stack.3), calls=%async_computation | async-start | bytes 8388608 | tf_op jit(solution)/shard_map/all_to_all | solution.py:142
  178.5 51.2 %copy-start.4 = (f32[512]{0:T(512)S(1)}, f32[512]{0:T(512)}, u32[]{:S(2)}) copy-start(f32[512]{0:T(512)} %param.15) | copy-start | bytes 6148
  236.5 23.2 %all-to-all-start.1 = ((f32[8,1,1024]{2,1,0:T(1,128)}), f32[8,1,1024]{2,1,0:T(1,128)S(1)}, u32[]{:S(2)}, u32[]{:S(2)}) async-start(f32[8,1,1024]{2,1,0:T(1,128)} %broadcast_in_dim.51), calls=%async_computation.1 | async-start | bytes 65536 | tf_op jit(solution)/shard_map/all_to_all | solution.py:23
Sparse Core Ops, SparseCore 0:
  10.1 137.3 all-gather.1
